TPU v7x, 256 devices: a whole 4x4x8 slice. The times are simulated.
256 devices in a mesh: tm: 8 (over x_hi, y), rows: 32 (over x_lo, z, core).
Axes of the slice: x: 4 (x_hi: 2, x_lo: 2; x = x_hi * 2 + x_lo), y: 4, z: 8, core: 2. Of those that a mesh axis runs over, the one named last changes fastest.
Arguments:
- record: bfloat16 [2, 65536, 4096], P(None, 'rows', 'tm'), may hold values from -6 to 6
- seed_list: int32 [4], replicated, may hold values from 0 to 65535
- block_offsets: int32 [2], replicated, may hold values from 0 to 1048575
Outputs:
- range_sketch: float32 [65536, 128], P('rows')
- corange_sketch: float32 [2, 256, 4096], P(None, 'rows', 'tm')
- core_sketch: float32 [384, 384], P('rows')
Inputs may be any that keep to these rules, and one draw needn't show every extreme that they name: `seed_list`: entries 0, 1, 2, 3 seed the range, co-range, core row and core column test matrices.
All inputs are finite; a program needn't handle non-finite values.
Results may differ from a plain program's by a relative error of at most 0.0041.
Values sent between devices are 32-bit elements; how exact they have to be, the bound alone decides.
A program may use at most 64 MiB of HBM per device.

v0:
```python
import math
import jax
import jax.numpy as jnp
from jax import lax
from jax.sharding import PartitionSpec as P

RANGE = 128
CORANGE = 256
CORE = 384


def in_blocks(x, dim, size):
    before, after = (x.shape[:dim], x.shape[dim + 1 :])
    return jnp.moveaxis(x.reshape(*before, size, -1, *after), dim, 0)


def sum_at_owner(x, axis, dim):
    parts = in_blocks(x, dim, lax.axis_size(axis))
    arrived = lax.all_to_all(parts, axis, split_axis=0, concat_axis=0, tiled=True)
    return arrived.sum(axis=0)


def from_everyone(x, axis):
    size = lax.axis_size(axis)
    return lax.all_to_all(jnp.broadcast_to(x[None], (size, *x.shape)), axis, 0, 0, tiled=True)


def taken_together(x, axis):
    return from_everyone(x, axis).sum(axis=0)


def shift_down(values, amount):
    return lax.shift_right_logical(values, jnp.full(values.shape, amount, jnp.int32))


def sketch_matrix(seed_value, first_ids, second_ids, factor):
    hashed = (
        first_ids[:, None] * 668265263 + second_ids[None, :] * 374761393 + seed_value * 625341585
    )
    hashed = jnp.bitwise_xor(hashed, shift_down(hashed, 15))
    hashed = hashed * 739982445
    hashed = jnp.bitwise_xor(hashed, shift_down(hashed, 12))
    hashed = hashed * 695872825
    hashed = jnp.bitwise_xor(hashed, shift_down(hashed, 15))
    byte_sum = jnp.bitwise_and(hashed, 255)
    byte_sum = byte_sum + jnp.bitwise_and(shift_down(hashed, 8), 255)
    byte_sum = byte_sum + jnp.bitwise_and(shift_down(hashed, 16), 255)
    byte_sum = byte_sum + jnp.bitwise_and(shift_down(hashed, 24), 255)
    return ((byte_sum - 510).astype(jnp.float32) * factor).astype(jnp.bfloat16)


def sum_range(part):
    return lax.psum(part, "tm")


def sum_corange(parts):
    return sum_at_owner(parts, "rows", 1)


def sum_core(part):
    share = sum_at_owner(part, "rows", 0)
    return taken_together(share, "tm")


def shards(record, seed_list, block_offsets):
    blocks, rows_dev, cols_dev = record.shape
    rows_count = lax.axis_size("rows")
    time_count = lax.axis_size("tm")
    row_factor = 1.0 / (147.8 * math.sqrt(rows_dev * rows_count))
    col_factor = 1.0 / (147.8 * math.sqrt(blocks * cols_dev * time_count))
    row_ids = lax.axis_index("rows") * rows_dev + jnp.arange(rows_dev, dtype=jnp.int32)
    psi_rows = sketch_matrix(
        seed_list[1], jnp.arange(CORANGE, dtype=jnp.int32), row_ids, row_factor
    )
    phi_rows = sketch_matrix(seed_list[2], jnp.arange(CORE, dtype=jnp.int32), row_ids, row_factor)
    col_base = lax.axis_index("tm") * cols_dev + jnp.arange(cols_dev, dtype=jnp.int32)
    range_local = jnp.zeros((rows_dev, RANGE), jnp.float32)
    core_local = jnp.zeros((CORE, CORE), jnp.float32)
    range_sketch = None
    core_sketch = None
    corange_parts = []
    for number in range(blocks):
        matrix = record[number]
        col_ids = block_offsets[number] + col_base
        omega_cols = sketch_matrix(
            seed_list[0], col_ids, jnp.arange(RANGE, dtype=jnp.int32), col_factor
        )
        xi_cols = sketch_matrix(
            seed_list[3], jnp.arange(CORE, dtype=jnp.int32), col_ids, col_factor
        )
        range_part = jnp.dot(matrix, omega_cols, preferred_element_type=jnp.float32)
        corange_part = jnp.dot(psi_rows, matrix, preferred_element_type=jnp.float32)
        projected = jnp.dot(phi_rows, matrix, preferred_element_type=jnp.float32)
        core_part = jnp.dot(
            projected, xi_cols.astype(jnp.float32).T, precision=lax.Precision.HIGHEST
        )
        range_local = range_local + range_part
        core_local = core_local + core_part
        corange_parts.append(corange_part)
    range_sketch = sum_range(range_local)
    core_sketch = sum_core(core_local)
    corange_sketch = sum_corange(jnp.stack(corange_parts))
    return (range_sketch, corange_sketch, core_sketch)


def solution(mesh):
    placed = (P(None, "rows", "tm"), P(), P())
    return jax.shard_map(
        shards,
        mesh=mesh,
        in_specs=placed,
        out_specs=(P("rows", None), P(None, "rows", "tm"), P("rows", None)),
        check_vma=False,
    )
```

profile of v0, /device:TPU:32, one launch (start us, length us, event | category | flops | bytes accessed | tf_op | source)
XLA Modules:
  0.0 185.7 jit_solution(12413052100564470267)
XLA Ops:
  7.2 1.5 fusion.175
  9.3 0.0 copy-start.1
  9.3 4.2 %fusion.9 = f32[384,512]{1,0:T(8,128)S(1)} fusion(bf16[2,2048,512]{2,1,0:T(8,128)(2,1)} %param.3, s32[]{:T(128)} %bitcast.12, s32[2048]{0:T(1024)S(1)} %add_multiply_fusion.1, s32[384]{0:T(512)S(1)} %iota_multiply_fusion), kind=kOutput, calls=%fused_computation.17 | convolution fusion | flops 824180736 | bytes 2893824 | tf_op jit(solution)/shard_map/dot_general | solution.py:93
  13.5 0.0 copy-done.1
  13.5 0.0 copy-start
  13.5 2.5 %fusion.12 = f32[384,512]{1,0:T(8,128)S(1)} fusion(bf16[2,2048,512]{2,1,0:T(8,128)(2,1)S(1)} %copy-done.1, s32[]{:T(128)} %bitcast.12, s32[2048]{0:T(1024)S(1)} %add_multiply_fusion.1, s32[384]{0:T(512)S(1)} %iota_multiply_fusion), kind=kOutput, calls=%fused_computation.20 | convolution fusion | flops 824180736 | bytes 2893828 | tf_op jit(solution)/shard_map/dot_general | solution.py:93
  16.0 0.0 copy-done
  16.0 0.6 fusion.176
  17.3 1.3 fusion.91
  18.6 1.4 fusion.32
  20.0 1.4 convolution_add_fusion.1
  21.3 0.9 reshape.121
  22.3 9.7 %all-to-all-start.1 = ((f32[32,12,384]{2,1,0:T(8,128)}), f32[32,12,384]{2,1,0:T(8,128)S(1)}, u32[]{:S(2)}, u32[]{:S(2)}) async-start(f32[32,12,384]{2,1,0:T(8,128)} %reshape.121), calls=%async_computation.1 | async-start | bytes 1572864 | tf_op jit(solution)/shard_map/all_to_all | solution.py:19
  32.6 0.0 copy-start.2
  32.6 3.4 %fusion.25 = f32[1,32,8,512]{3,2,1,0:T(8,128)S(1)} fusion(bf16[2,2048,512]{2,1,0:T(8,128)(2,1)} %param.3, s32[]{:T(128)} %bitcast.6, s32[2048]{0:T(1024)S(1)} %add_multiply_fusion.1, s32[32,8]{1,0:T(8,128)S(1)} %add_multiply_fusion), kind=kOutput, calls=%fused_computation.33 | convolution fusion | flops 549453824 | bytes 2631168 | tf_op jit(solution)/shard_map/dot_general | solution.py:92
  36.0 0.0 copy-done.2
  36.0 1.7 fusion.22
  37.7 17.6 %all-to-all-done.1 = f32[32,12,384]{2,1,0:T(8,128)S(1)} async-done(((f32[32,12,384]{2,1,0:T(8,128)}), f32[32,12,384]{2,1,0:T(8,128)S(1)}, u32[]{:S(2)}, u32[]{:S(2)}) %all-to-all-start.1) | async-done | bytes 589856 | tf_op jit(solution)/shard_map/all_to_all | solution.py:19
  55.3 0.1 reduce_sum.28
  55.4 0.7 broadcast_in_dim.50
  56.0 6.6 %all-to-all-start.2 = ((f32[8,12,384]{2,1,0:T(8,128)}), f32[8,12,384]{2,1,0:T(8,128)S(1)}, u32[]{:S(2)}, u32[]{:S(2)}) async-start(f32[8,12,384]{2,1,0:T(8,128)} %broadcast_in_dim.50), calls=%async_computation.2 | async-start | bytes 393216 | tf_op jit(solution)/shard_map/all_to_all | solution.py:25
  62.7 0.1 maximum_bitcast_fusion
  62.8 1.1 copy.12
  63.8 7.3 %all-to-all-done.2 = f32[8,12,384]{2,1,0:T(8,128)S(1)} async-done(((f32[8,12,384]{2,1,0:T(8,128)}), f32[8,12,384]{2,1,0:T(8,128)S(1)}, u32[]{:S(2)}, u32[]{:S(2)}) %all-to-all-start.2) | async-done | bytes 147488 | tf_op jit(solution)/shard_map/all_to_all | solution.py:25
  71.1 3.8 %all-to-all-start = ((f32[32,2,8,512]{3,2,1,0:T(8,128)}), f32[32,2,8,512]{3,2,1,0:T(8,128)S(1)}, u32[]{:S(2)}, u32[]{:S(2)}) async-start(f32[32,2,8,512]{3,2,1,0:T(8,128)} %copy.12), calls=%async_computation | async-start | bytes 2097152 | tf_op jit(solution)/shard_map/all_to_all | solution.py:19
  74.9 0.0 all-reduce.2.cloned.1.call-start
  75.6 1.3 fusion.92
  76.9 2.6 %fusion.14 = f32[128,2048]{1,0:T(8,128)S(1)} fusion(bf16[2,2048,512]{2,1,0:T(8,128)(2,1)} %param.3, s32[]{:T(128)} %bitcast.1, s32[128]{0:T(128)S(1)} %iota_multiply_fusion.1, s32[512]{0:T(512)S(1)} %get-tuple-element.26), kind=kOutput, calls=%fused_computation.22 | convolution fusion | flops 270008320 | bytes 3148800 | tf_op jit(solution)/shard_map/dot_general | solution.py:91
  79.5 3.6 %fusion.2 = f32[2048,128]{0,1:T(8,128)} fusion(f32[128,2048]{1,0:T(8,128)S(1)} %fusion.14, bf16[2,2048,512]{2,1,0:T(8,128)(2,1)} %param.3, s32[512]{0:T(512)S(1)} %get-tuple-element.27, s32[]{:T(128)} %bitcast.1, s32[128]{0:T(128)S(1)} %iota_multiply_fusion.1), kind=kOutput, calls=%fused_computation.10 | convolution fusion | flops 270270464 | bytes 4197376 | tf_op jit(solution)/shard_map/dot_general | solution.py:91
  83.1 0.0 all-reduce.2.cloned.1.call-update
  83.2 91.9 %all-reduce.2.cloned.1.call-done = f32[2048,128]{0,1:T(8,128)} async-done(((f32[2048,128]{0,1:T(8,128)}), f32[2048,128]{0,1:T(8,128)}) %all-reduce.2.cloned.1.call-update) | async-done | bytes 1048592 | tf_op jit(solution)/shard_map/psum | solution.py:53
  175.0 2.5 %copy.14 = f32[2048,128]{1,0:T(8,128)} copy(f32[2048,128]{0,1:T(8,128)} %all-reduce.2.cloned.1.call-done) | data formatting | bytes 2097152
  177.6 0.6 reduce_sum.29
  178.2 0.0 all-to-all-done
  178.2 0.7 reduce_sum.27
  (4 shorter events, 0.0 us)
Async XLA Ops:
  9.3 4.2 %copy-start.1 = (bf16[2,2048,512]{2,1,0:T(8,128)(2,1)S(1)}, bf16[2,2048,512]{2,1,0:T(8,128)(2,1)}, u32[]{:S(2)}) copy-start(bf16[2,2048,512]{2,1,0:T(8,128)(2,1)} %param.3) | copy-start | bytes 12582916
  13.5 2.5 %copy-start = (s32[2]{0:T(128)S(1)}, s32[2]{0:T(128)}, u32[]{:S(2)}) copy-start(s32[2]{0:T(128)} %param.5) | copy-start | bytes 28
  22.3 33.0 %all-to-all-start.1 = ((f32[32,12,384]{2,1,0:T(8,128)}), f32[32,12,384]{2,1,0:T(8,128)S(1)}, u32[]{:S(2)}, u32[]{:S(2)}) async-start(f32[32,12,384]{2,1,0:T(8,128)} %reshape.121), calls=%async_computation.1 | async-start | bytes 1572864 | tf_op jit(solution)/shard_map/all_to_all | solution.py:19
  32.6 3.4 %copy-start.2 = (bf16[2,2048,512]{2,1,0:T(8,128)(2,1)S(1)}, bf16[2,2048,512]{2,1,0:T(8,128)(2,1)}, u32[]{:S(2)}) copy-start(bf16[2,2048,512]{2,1,0:T(8,128)(2,1)} %param.3) | copy-start | bytes 12582916
  56.0 15.1 %all-to-all-start.2 = ((f32[8,12,384]{2,1,0:T(8,128)}), f32[8,12,384]{2,1,0:T(8,128)S(1)}, u32[]{:S(2)}, u32[]{:S(2)}) async-start(f32[8,12,384]{2,1,0:T(8,128)} %broadcast_in_dim.50), calls=%async_computation.2 | async-start | bytes 393216 | tf_op jit(solution)/shard_map/all_to_all | solution.py:25
  71.1 107.1 %all-to-all-start = ((f32[32,2,8,512]{3,2,1,0:T(8,128)}), f32[32,2,8,512]{3,2,1,0:T(8,128)S(1)}, u32[]{:S(2)}, u32[]{:S(2)}) async-start(f32[32,2,8,512]{3,2,1,0:T(8,128)} %copy.12), calls=%async_computation | async-start | bytes 2097152 | tf_op jit(solution)/shard_map/all_to_all | solution.py:19
  74.9 100.1 %all-reduce.2.cloned.1.call-start = ((), (), s32[]{:S(2)}) async-start(), calls=%async_computation.3 | async-start | bytes 2097152 | tf_op jit(solution)/shard_map/psum | solution.py:53
Sparse Core Ops, SparseCore 0:
  83.3 91.7 all-reduce.1
where the time goes:
time: 186 us
  waiting for transfers between devices  117 us (63%)
  matrix products  20.8 us (11%)
  starting transfers between devices  20.1 us (11%)
  between operations  16.8 us (9%)
  local copies, waits for them, and re-layouts  7.35 us (4%)
  other arithmetic  3.97 us (2%)
    psum x1, waiting for transfers between devices, sum_range(): return lax.psum(part, 'tm')  91.9 us
    all_to_all x2, waiting for transfers between devices, sum_at_owner(): lax.all_to_all(parts, axis, split_axis=0, concat_axis=0, tiled=True)  17.6 us
    all_to_all x2, starting transfers between devices, sum_at_owner(): lax.all_to_all(parts, axis, split_axis=0, concat_axis=0, tiled=True)  13.4 us
    all_to_all x1, waiting for transfers between devices, from_everyone(): lax.all_to_all(jnp.broadcast_to(x[None], (size, *x.shape)), axis, 0, 0, t...  7.3 us
    dot_general x2, matrix products, shards(): projected = jnp.dot(phi_rows, matrix, preferred_element_type=jnp.float32)  6.71 us
    all_to_all x1, starting transfers between devices, from_everyone(): lax.all_to_all(jnp.broadcast_to(x[None], (size, *x.shape)), axis, 0, 0, t...  6.64 us
    dot_general x2, matrix products, shards(): range_part = jnp.dot(matrix, omega_cols, preferred_element_type=jnp.float32)  6.24 us
    dot_general x2, matrix products, shards(): corange_part = jnp.dot(psi_rows, matrix, preferred_element_type=jnp.float32)  5.1 us
  transfers between devices with their start and end apart: 4, of which 3 were waited for; matrix products, arithmetic and copies ran while one was open for 9% of the time, Pallas kernels for 0%

commit v1 on v0

--- a/solution.py
+++ b/solution.py
@@ -50,7 +50,7 @@
 
 
 def sum_range(part):
-    return lax.psum(part, "tm")
+    return lax.all_gather(part, "tm").sum(axis=0)
 
 
 def sum_corange(parts):

time: 186 us -> 171 us (0.919)
  waiting for transfers between devices: 117 us -> 89.3 us
  local copies, waits for them, and re-layouts: 7.35 us -> 17.6 us
  other arithmetic: 3.97 us -> 6.17 us
    psum x1 -> x0, waiting for transfers between devices: 91.9 us -> none  [sum_range(): return lax.psum(part, 'tm')]
    all_gather x0 -> x1, waiting for transfers between devices: none -> 35.2 us  [sum_range(): return lax.all_gather(part, 'tm').sum(axis=0)]
    all_to_all x2, waiting for transfers between devices: 17.6 us -> 45.7 us  [sum_at_owner(): lax.all_to_all(parts, axis, split_axis=0, concat_axis=0, tiled=True)]
    unnamed x7 -> x6, local copies, waits for them, and re-layouts: 2.55 us -> 12 us
    reduce_sum x0 -> x1, other arithmetic: none -> 2.1 us  [sum_range(): return lax.all_gather(part, 'tm').sum(axis=0)]
  transfers between devices with their start and end apart: 4 -> 4, of which waited for: 3 -> 4; matrix products, arithmetic and copies ran while one was open for 9% -> 12% of each run, Pallas kernels for 0% -> 0%
where the time goes in v1:
time: 171 us; the launch traced here: 170 us
  waiting for transfers between devices  89.3 us (52%)
  matrix products  20.6 us (12%)
  starting transfers between devices  20.1 us (12%)
  local copies, waits for them, and re-layouts  17.6 us (10%)
  between operations  16.6 us (10%)
  other arithmetic  6.17 us (4%)
    all_to_all x2, waiting for transfers between devices, sum_at_owner(): lax.all_to_all(parts, axis, split_axis=0, concat_axis=0, tiled=True)  45.7 us
    all_gather x1, waiting for transfers between devices, sum_range(): return lax.all_gather(part, 'tm').sum(axis=0)  35.2 us
    all_to_all x2, starting transfers between devices, sum_at_owner(): lax.all_to_all(parts, axis, split_axis=0, concat_axis=0, tiled=True)  13.4 us
    unnamed x6, local copies, waits for them, and re-layouts  12 us
    all_to_all x1, waiting for transfers between devices, from_everyone(): lax.all_to_all(jnp.broadcast_to(x[None], (size, *x.shape)), axis, 0, 0, t...  8.37 us
    all_to_all x1, starting transfers between devices, from_everyone(): lax.all_to_all(jnp.broadcast_to(x[None], (size, *x.shape)), axis, 0, 0, t...  6.64 us
    dot_general x2, matrix products, shards(): projected = jnp.dot(phi_rows, matrix, preferred_element_type=jnp.float32)  6.56 us
    dot_general x2, matrix products, shards(): range_part = jnp.dot(matrix, omega_cols, preferred_element_type=jnp.float32)  6.21 us
  transfers between devices with their start and end apart: 4, of which 4 were waited for; matrix products, arithmetic and copies ran while one was open for 12% of the time, Pallas kernels for 0%

profile of v1, /device:TPU:32, one launch (start us, length us, event | category | flops | bytes accessed | tf_op | source)
XLA Modules:
  0.0 170.4 jit_solution(11775754372544489531)
XLA Ops:
  7.2 0.0 all-gather.3.cloned.1.call-start
  7.2 1.4 fusion.175
  8.6 1.4 fusion.176
  10.7 1.3 fusion.92
  12.0 2.6 %fusion.14 = f32[128,2048]{1,0:T(8,128)S(1)} fusion(bf16[2,2048,512]{2,1,0:T(8,128)(2,1)} %param.3, s32[]{:T(128)} %bitcast.1, s32[128]{0:T(128)S(1)} %iota_multiply_fusion.1, s32[512]{0:T(512)S(1)} %get-tuple-element.20), kind=kOutput, calls=%fused_computation.23 | convolution fusion | flops 270008320 | bytes 3148800 | tf_op jit(solution)/shard_map/dot_general | solution.py:91
  14.6 3.6 %fusion.2 = f32[2048,128]{0,1:T(8,128)} fusion(f32[128,2048]{1,0:T(8,128)S(1)} %fusion.14, bf16[2,2048,512]{2,1,0:T(8,128)(2,1)} %param.3, s32[512]{0:T(512)S(1)} %get-tuple-element.21, s32[]{:T(128)} %bitcast.1, s32[128]{0:T(128)S(1)} %iota_multiply_fusion.1), kind=kOutput, calls=%fused_computation.11 | convolution fusion | flops 270270464 | bytes 4197376 | tf_op jit(solution)/shard_map/dot_general | solution.py:91
  18.2 0.0 all-gather.3.cloned.1.call-update
  19.4 1.3 fusion.91
  20.7 4.1 %fusion.12 = f32[384,512]{1,0:T(8,128)S(1)} fusion(bf16[2,2048,512]{2,1,0:T(8,128)(2,1)} %param.3, s32[]{:T(128)} %bitcast.12, s32[2048]{0:T(1024)S(1)} %add_multiply_fusion.1, s32[384]{0:T(512)S(1)} %iota_multiply_fusion), kind=kOutput, calls=%fused_computation.21 | convolution fusion | flops 824180736 | bytes 2893824 | tf_op jit(solution)/shard_map/dot_general | solution.py:93
  24.8 0.0 copy-start
  24.8 1.3 fusion.32
  26.2 0.8 copy-done
  27.0 2.5 %fusion.9 = f32[384,512]{1,0:T(8,128)S(1)} fusion(bf16[2,2048,512]{2,1,0:T(8,128)(2,1)S(1)} %copy-done, s32[]{:T(128)} %bitcast.12, s32[2048]{0:T(1024)S(1)} %add_multiply_fusion.1, s32[384]{0:T(512)S(1)} %iota_multiply_fusion), kind=kOutput, calls=%fused_computation.18 | convolution fusion | flops 824180736 | bytes 2893828 | tf_op jit(solution)/shard_map/dot_general | solution.py:93
  29.5 1.4 convolution_add_fusion.1
  30.8 1.0 reshape.121
  31.8 9.7 %all-to-all-start.1 = ((f32[32,12,384]{2,1,0:T(8,128)}), f32[32,12,384]{2,1,0:T(8,128)S(1)}, u32[]{:S(2)}, u32[]{:S(2)}) async-start(f32[32,12,384]{2,1,0:T(8,128)} %reshape.121), calls=%async_computation.1 | async-start | bytes 1572864 | tf_op jit(solution)/shard_map/all_to_all | solution.py:19
  42.2 0.0 copy-start.1
  42.2 3.4 %fusion.25 = f32[1,32,8,512]{3,2,1,0:T(8,128)S(1)} fusion(bf16[2,2048,512]{2,1,0:T(8,128)(2,1)} %param.3, s32[]{:T(128)} %bitcast.6, s32[2048]{0:T(1024)S(1)} %add_multiply_fusion.1, s32[32,8]{1,0:T(8,128)S(1)} %add_multiply_fusion), kind=kOutput, calls=%fused_computation.34 | convolution fusion | flops 549453824 | bytes 2631168 | tf_op jit(solution)/shard_map/dot_general | solution.py:92
  45.6 0.0 copy-done.1
  45.6 1.7 fusion.22
  47.3 17.6 %all-to-all-done.1 = f32[32,12,384]{2,1,0:T(8,128)S(1)} async-done(((f32[32,12,384]{2,1,0:T(8,128)}), f32[32,12,384]{2,1,0:T(8,128)S(1)}, u32[]{:S(2)}, u32[]{:S(2)}) %all-to-all-start.1) | async-done | bytes 589856 | tf_op jit(solution)/shard_map/all_to_all | solution.py:19
  64.9 0.1 reduce_sum.38
  64.9 0.7 broadcast_in_dim.50
  65.6 6.6 %all-to-all-start.2 = ((f32[8,12,384]{2,1,0:T(8,128)}), f32[8,12,384]{2,1,0:T(8,128)S(1)}, u32[]{:S(2)}, u32[]{:S(2)}) async-start(f32[8,12,384]{2,1,0:T(8,128)} %broadcast_in_dim.50), calls=%async_computation.2 | async-start | bytes 393216 | tf_op jit(solution)/shard_map/all_to_all | solution.py:25
  72.2 0.1 maximum_bitcast_fusion
  72.3 1.1 copy.10
  73.5 8.4 %all-to-all-done.2 = f32[8,12,384]{2,1,0:T(8,128)S(1)} async-done(((f32[8,12,384]{2,1,0:T(8,128)}), f32[8,12,384]{2,1,0:T(8,128)S(1)}, u32[]{:S(2)}, u32[]{:S(2)}) %all-to-all-start.2) | async-done | bytes 147488 | tf_op jit(solution)/shard_map/all_to_all | solution.py:25
  81.8 3.7 %all-to-all-start = ((f32[32,2,8,512]{3,2,1,0:T(8,128)}), f32[32,2,8,512]{3,2,1,0:T(8,128)S(1)}, u32[]{:S(2)}, u32[]{:S(2)}) async-start(f32[32,2,8,512]{3,2,1,0:T(8,128)} %copy.10), calls=%async_computation | async-start | bytes 2097152 | tf_op jit(solution)/shard_map/all_to_all | solution.py:19
  85.6 0.6 reduce_sum.39
  86.2 28.2 %all-to-all-done = f32[32,2,8,512]{3,2,1,0:T(8,128)S(1)} async-done(((f32[32,2,8,512]{3,2,1,0:T(8,128)}), f32[32,2,8,512]{3,2,1,0:T(8,128)S(1)}, u32[]{:S(2)}, u32[]{:S(2)}) %all-to-all-start) | async-done | bytes 1048608 | tf_op jit(solution)/shard_map/all_to_all | solution.py:19
  114.4 0.7 reduce_sum.37
  115.1 35.2 %all-gather.3.cloned.1.call-done = f32[16384,128]{0,1:T(8,128)} async-done(((f32[2048,128]{0,1:T(8,128)}), f32[16384,128]{0,1:T(8,128)}) %all-gather.3.cloned.1.call-update) | async-done | bytes 8388624 | tf_op jit(solution)/shard_map/all_gather | solution.py:53
  150.3 9.9 %copy.14 = f32[16,8,8,2048]{3,2,1,0:T(8,128)S(1)} copy(f32[16,8,8,2048]{3,1,2,0:T(8,128)} %bitcast.41) | data formatting | bytes 16777216
  160.1 2.1 %bitcast_reduce_fusion = f32[2048,128]{0,1:T(8,128)S(1)} fusion(f32[16,8,8,2048]{3,2,1,0:T(8,128)S(1)} %copy.14), kind=kLoop, calls=%fused_computation | loop fusion | flops 1835008 | bytes 9437184 | tf_op jit(solution)/shard_map/reduce_sum | solution.py:53
  162.2 1.3 copy.12
  (4 shorter events, 0.0 us)
Async XLA Ops:
  7.2 143.1 %all-gather.3.cloned.1.call-start = ((), (), s32[]{:S(2)}) async-start(), calls=%async_computation.3 | async-start | bytes 9437184 | tf_op jit(solution)/shard_map/all_gather | solution.py:53
  24.8 2.2 %copy-start = (bf16[2,2048,512]{2,1,0:T(8,128)(2,1)S(1)}, bf16[2,2048,512]{2,1,0:T(8,128)(2,1)}, u32[]{:S(2)}) copy-start(bf16[2,2048,512]{2,1,0:T(8,128)(2,1)} %param.3) | copy-start | bytes 12582916
  31.8 33.0 %all-to-all-start.1 = ((f32[32,12,384]{2,1,0:T(8,128)}), f32[32,12,384]{2,1,0:T(8,128)S(1)}, u32[]{:S(2)}, u32[]{:S(2)}) async-start(f32[32,12,384]{2,1,0:T(8,128)} %reshape.121), calls=%async_computation.1 | async-start | bytes 1572864 | tf_op jit(solution)/shard_map/all_to_all | solution.py:19
  42.2 3.4 %copy-start.1 = (bf16[2,2048,512]{2,1,0:T(8,128)(2,1)S(1)}, bf16[2,2048,512]{2,1,0:T(8,128)(2,1)}, u32[]{:S(2)}) copy-start(bf16[2,2048,512]{2,1,0:T(8,128)(2,1)} %param.3) | copy-start | bytes 12582916
  65.6 16.2 %all-to-all-start.2 = ((f32[8,12,384]{2,1,0:T(8,128)}), f32[8,12,384]{2,1,0:T(8,128)S(1)}, u32[]{:S(2)}, u32[]{:S(2)}) async-start(f32[8,12,384]{2,1,0:T(8,128)} %broadcast_in_dim.50), calls=%async_computation.2 | async-start | bytes 393216 | tf_op jit(solution)/shard_map/all_to_all | solution.py:25
  81.8 32.5 %all-to-all-start = ((f32[32,2,8,512]{3,2,1,0:T(8,128)}), f32[32,2,8,512]{3,2,1,0:T(8,128)S(1)}, u32[]{:S(2)}, u32[]{:S(2)}) async-start(f32[32,2,8,512]{3,2,1,0:T(8,128)} %copy.10), calls=%async_computation | async-start | bytes 2097152 | tf_op jit(solution)/shard_map/all_to_all | solution.py:19
Sparse Core Ops, SparseCore 0:
  18.3 131.8 all-gather.2
